TPU v7x, 32 devices: a whole 2x2x4 slice. The times are simulated.
32 devices in a mesh: frame: 4 (over z), row: 8 (over y, x, core).
Axes of the slice: x: 2, y: 2, z: 4, core: 2. Of those that a mesh axis runs over, the one named last changes fastest.
Arguments:
- fine: bfloat16 [8, 320, 32, 128], P('frame', None, 'row'), may hold values from -6 to 6
- coarse: bfloat16 [4, 64, 1280], P(None, 'row', 'frame'), may hold values from -6 to 6
- w_qkv: bfloat16 [3, 1280, 1280], P(None, None, 'frame'), may hold values from -0.15625 to 0.15625
- w_out: bfloat16 [1280, 1280], P('frame'), may hold values from -0.15625 to 0.15625
- w_up: bfloat16 [1280, 320], P('frame'), may hold values from -0.15625 to 0.15625
- gain_one: float32 [320], replicated, may hold values from 0.1 to 1.9
- conv_space: bfloat16 [3, 3, 320, 320], replicated, may hold values from -0.109375 to 0.109375
- gain_two: float32 [320], replicated, may hold values from 0.1 to 1.9
- conv_time: bfloat16 [3, 320, 320], replicated, may hold values from -0.1875 to 0.1875
Outputs:
- result: bfloat16 [8, 320, 32, 128], P('frame', None, 'row')
All inputs are finite; a program needn't handle non-finite values.
Results may differ from a plain program's by a relative error of at most 0.013.
Values may be sent and summed in bfloat16 or wider, within the bound.
A program may use at most 64 MiB of HBM per device.

v0:
```python
import math

import jax
import jax.numpy as jnp
from jax import lax
from jax.sharding import PartitionSpec as P

HD = 80


def from_partner(value, axis, apart):
    mask = 2**apart
    pairs = [(source, source ^ mask) for source in range(lax.axis_size(axis))]
    return lax.ppermute(value, axis, pairs)


def with_halo(cells, sides, width):
    for axis, dim in sides:
        count = lax.axis_size(axis)
        ends = count - 1
        head = lax.slice_in_dim(cells, 0, width, axis=dim)
        tail = lax.slice_in_dim(cells, cells.shape[dim] - width, cells.shape[dim], axis=dim)
        cells = jnp.concatenate(
            [
                lax.ppermute(tail, axis, [(i, (i + 1) % count) for i in range(ends)]),
                cells,
                lax.ppermute(head, axis, [((i + 1) % count, i) for i in range(ends)]),
            ],
            axis=dim,
        )
    return cells


def norm_silu(values, gain):
    square = jnp.mean(values * values, axis=1, keepdims=True)
    scaled = values * lax.rsqrt(square + 1e-06) * gain[None, :, None, None]
    return jax.nn.silu(scaled).astype(jnp.bfloat16)


def convolve_space(extended, conv_space):
    padded = jnp.pad(extended, ((0, 0), (0, 0), (0, 0), (1, 1)))
    rows_here = extended.shape[2] - 2
    width = extended.shape[3]
    spatial = None
    for offset_y in range(3):
        for offset_x in range(3):
            window = padded[:, :, offset_y : offset_y + rows_here, offset_x : offset_x + width]
            term = jnp.einsum(
                "fcrw,cd->fdrw",
                window,
                conv_space[offset_y, offset_x],
                preferred_element_type=jnp.float32,
            )
            spatial = term if spatial is None else spatial + term
    return spatial


def local(fine, coarse, w_qkv, w_out, w_up, gain_one, conv_space, gain_two, conv_time):
    frame_count = lax.axis_size("frame")
    f_dev = fine.shape[0]
    width = fine.shape[3]
    cf_count, p_dev, c_dev = coarse.shape
    heads_local = w_qkv.shape[2] // HD
    qkv = jnp.einsum(
        "fpc,icd->ifpd",
        lax.all_gather(coarse, "frame", axis=2, tiled=True),
        w_qkv,
        preferred_element_type=jnp.float32,
    ).astype(jnp.bfloat16)
    query = qkv[0].reshape(cf_count, p_dev, heads_local, HD)
    keys = qkv[1].reshape(cf_count, p_dev, heads_local, HD)
    values = qkv[2].reshape(cf_count, p_dev, heads_local, HD)
    scores = jnp.einsum(
        "fphd,gphd->phfg", query, keys, preferred_element_type=jnp.float32
    ) / math.sqrt(HD)
    probs = jax.nn.softmax(scores, axis=-1).astype(jnp.bfloat16)
    attn = jnp.einsum("phfg,gphd->fphd", probs, values, preferred_element_type=jnp.float32).astype(
        jnp.bfloat16
    )
    attn = attn.reshape(cf_count * p_dev, heads_local * HD)
    partial_out = jnp.dot(attn, w_out, preferred_element_type=jnp.float32).reshape(
        cf_count, p_dev, -1
    )
    share = lax.psum_scatter(partial_out, "frame", scatter_dimension=2, tiled=True)
    coarse_out = (coarse.astype(jnp.float32) + share).astype(jnp.bfloat16)
    up_partial = jnp.einsum("fpc,cd->fpd", coarse_out, w_up, preferred_element_type=jnp.float32)
    up_cells = lax.psum(up_partial, "frame").astype(jnp.bfloat16)
    partner = from_partner(up_cells, "row", 0)
    is_even = lax.axis_index("row") % 2 == 0
    coarse_row = jnp.where(
        is_even,
        jnp.concatenate([up_cells, partner], axis=1),
        jnp.concatenate([partner, up_cells], axis=1),
    )
    global_frames = lax.axis_index("frame") * f_dev + jnp.arange(f_dev, dtype=jnp.int32)
    target = global_frames * cf_count // (f_dev * frame_count)
    select = (target[:, None] == jnp.arange(cf_count, dtype=jnp.int32)[None, :]).astype(jnp.float32)
    picked = jnp.einsum("tk,kwc->tcw", select, coarse_row.astype(jnp.float32))
    widened = jnp.repeat(picked, width // picked.shape[2], axis=2)
    merged = (fine.astype(jnp.float32) + widened[:, :, None, :]).astype(jnp.bfloat16)
    first = norm_silu(merged.astype(jnp.float32), gain_one)
    extended = with_halo(first, (("row", 2),), 1)
    second = norm_silu(convolve_space(extended, conv_space), gain_two)
    second_ext = with_halo(second, (("frame", 0),), 1)
    temporal = None
    for offset in range(3):
        term = jnp.einsum(
            "fcrw,cd->fdrw",
            second_ext[offset : offset + f_dev],
            conv_time[offset],
            preferred_element_type=jnp.float32,
        )
        temporal = term if temporal is None else temporal + term
    return (merged.astype(jnp.float32) + temporal).astype(jnp.bfloat16)


def solution(mesh):
    return jax.shard_map(
        local,
        mesh=mesh,
        in_specs=(
            P("frame", None, "row", None),
            P(None, "row", "frame"),
            P(None, None, "frame"),
            P("frame", None),
            P("frame", None),
            P(),
            P(),
            P(),
            P(),
        ),
        out_specs=P("frame", None, "row", None),
        check_vma=False,
    )
```

profile of v0, /device:TPU:11, one launch (start us, length us, event | category | flops | bytes accessed | tf_op | source)
XLA Modules:
  0.0 131.6 jit_solution(14206423180547574291)
XLA Ops:
  6.5 1.1 copy.53
  7.6 24.7 %all_gather.3 = bf16[4,8,1280]{1,0,2:T(4,128)(2,1)} all-gather(bf16[4,8,320]{1,0,2:T(4,128)(2,1)S(1)} %copy.53), channel_id=1, replica_groups=mesh['frame'=4,'row'=8] {'frame'}, dimensions={2}, use_global_device_ids=true | all-gather | bytes 102400 | tf_op jit(solution)/shard_map/all_gather | solution.py:66
  32.3 1.7 %copy.54 = bf16[4,8,1280]{2,1,0:T(8,128)(2,1)S(1)} copy(bf16[4,8,1280]{1,0,2:T(4,128)(2,1)} %all_gather.3) | data formatting | bytes 163840 | tf_op jit(solution)/shard_map/all_gather | solution.py:66
  34.0 0.8 fusion.34
  34.8 0.1 reshape_squeeze.10
  34.9 0.1 reshape_squeeze.11
  35.0 0.1 reshape_squeeze.9
  35.1 0.2 fusion.123
  35.3 0.4 fusion.38
  35.8 0.1 dot_general.59
  35.9 1.4 %fusion.39 = f32[4,8,1280]{2,1,0:T(8,128)S(1)} fusion(bf16[4,8,320]{2,1,0:T(8,128)(2,1)S(1)} %dot_general.59, bf16[320,1280]{1,0:T(8,128)(2,1)} %param.12), kind=kOutput, calls=%fused_computation.50 | convolution fusion | flops 26214400 | bytes 1003520 | tf_op jit(solution)/shard_map/dot_general | solution.py:81
  37.2 1.9 %copy.90 = f32[4,8,1280]{1,0,2:T(4,128)} copy(f32[4,8,1280]{2,1,0:T(8,128)S(1)} %fusion.39) | data formatting | bytes 327680
  39.2 3.3 %reshape.62 = f32[1280,32]{1,0:T(8,128)} reshape(f32[1280,4,8]{2,1,0:T(4,128)} %bitcast.157) | data formatting | bytes 327680
  42.5 0.0 reduce-scatter.4.cloned.1.call-update
  42.5 21.9 %reduce-scatter.4.cloned.1.call-done = f32[320,32]{1,0:T(8,128)} async-done(((f32[1280,32]{1,0:T(8,128)}), f32[320,32]{1,0:T(8,128)}) %reduce-scatter.4.cloned.1.call-update) | async-done | bytes 40976
  64.4 2.1 %reshape.63 = f32[320,4,8]{2,1,0:T(4,128)} reshape(f32[320,32]{1,0:T(8,128)} %reduce-scatter.4.cloned.1.call-done) | data formatting | bytes 81920
  66.5 1.4 %copy.91 = f32[4,8,320]{2,1,0:T(8,128)S(1)} copy(f32[4,8,320]{1,0,2:T(4,128)} %bitcast.158) | data formatting | bytes 81920
  67.8 0.2 fusion.72
  68.0 12.8 %psum.7 = bf16[4,8,320]{2,1,0:T(8,128)(2,1)S(1)} all-reduce(f32[4,8,320]{2,1,0:T(8,128)S(1)} %fusion.72), channel_id=1, replica_groups=mesh['frame'=4,'row'=8] {'frame'}, use_global_device_ids=true, to_apply=%region_3.0 | all-reduce | flops 10240 | bytes 61440 | tf_op jit(solution)/shard_map/psum | solution.py:87
  80.8 6.1 %collective-permute-start = (bf16[4,8,320]{2,1,0:T(8,128)(2,1)S(1)}, bf16[4,8,320]{2,1,0:T(8,128)(2,1)S(1)}, u32[]{:S(2)}, u32[]{:S(2)}) collective-permute-start(bf16[4,8,320]{2,1,0:T(8,128)(2,1)S(1)} %psum.7), channel_id=1, source_target_pairs={{0,1},{1,0},{2,3},{3,2},{4,5},{5,4},{6,7},{7,6},{8,9},{9,8},{10,11... | collective-permute-start | bytes 61448 | tf_op jit(solution)/shard_map/ppermute | solution.py:14
  87.0 0.8 collective-permute-done
  87.8 0.2 convolution_bitcast_fusion
  88.0 0.8 broadcast_bitcast_fusion
  88.8 1.2 copy.62
  90.0 0.1 fusion.18
  90.2 0.5 fusion.25
  90.7 3.4 %collective-permute-start.1 = (bf16[2,320,1,128]{3,1,2,0:T(8,128)(2,1)S(1)}, bf16[2,320,1,128]{3,1,2,0:T(8,128)(2,1)S(1)}, u32[]{:S(2)}, u32[]{:S(2)}) collective-permute-start(bf16[2,320,1,128]{3,1,2,0:T(8,128)(2,1)S(1)} %get-tuple-element.7), channel_id=1, source_target_pairs={{0,1},{1,2},{2,3},{3,4},{4,5},{5,6},{6,7},{8,9},{9,10},{10,11},{11... | collective-permute-start | bytes 491528 | tf_op jit(solution)/shard_map/ppermute | solution.py:25
  94.0 1.9 %collective-permute-start.2 = (bf16[2,320,1,128]{3,1,2,0:T(8,128)(2,1)S(1)}, bf16[2,320,1,128]{3,1,2,0:T(8,128)(2,1)S(1)}, u32[]{:S(2)}, u32[]{:S(2)}) collective-permute-start(bf16[2,320,1,128]{3,1,2,0:T(8,128)(2,1)S(1)} %get-tuple-element.8), channel_id=1, source_target_pairs={{1,0},{2,1},{3,2},{4,3},{5,4},{6,5},{7,6},{9,8},{10,9},{11,10},{12... | collective-permute-start | bytes 491528 | tf_op jit(solution)/shard_map/ppermute | solution.py:27
  96.0 0.5 fusion.66
  96.5 5.1 %collective-permute-done.2 = bf16[2,320,1,128]{3,1,2,0:T(8,128)(2,1)S(1)} collective-permute-done((bf16[2,320,1,128]{3,1,2,0:T(8,128)(2,1)S(1)}, bf16[2,320,1,128]{3,1,2,0:T(8,128)(2,1)S(1)}, u32[]{:S(2)}, u32[]{:S(2)}) %collective-permute-start.2) | collective-permute-done | bytes 163872 | tf_op jit(solution)/shard_map/ppermute | solution.py:27
  101.6 1.0 fusion.8
  102.6 0.5 fusion.51
  103.1 0.7 fusion.53
  103.8 0.7 fusion.44
  104.5 0.5 fusion.48
  105.0 0.5 fusion.55
  105.5 0.6 fusion.16
  106.1 0.5 fusion.46
  106.6 1.0 multiply_reduce_fusion
  107.6 0.5 fusion.29
  108.2 4.7 %collective-permute-start.4 = (bf16[1,320,4,128]{3,1,2,0:T(8,128)(2,1)S(1)}, bf16[1,320,4,128]{3,1,2,0:T(8,128)(2,1)S(1)}, u32[]{:S(2)}, u32[]{:S(2)}) collective-permute-start(bf16[1,320,4,128]{3,1,2,0:T(8,128)(2,1)S(1)} %get-tuple-element.6), channel_id=1, source_target_pairs={{8,0},{16,8},{24,16},{9,1},{17,9},{25,17},{10,2},{18,10},{26,18},{... | collective-permute-start | bytes 983048 | tf_op jit(solution)/shard_map/ppermute | solution.py:27
  112.9 1.9 %collective-permute-start.3 = (bf16[1,320,4,128]{3,1,2,0:T(8,128)(2,1)S(1)}, bf16[1,320,4,128]{3,1,2,0:T(8,128)(2,1)S(1)}, u32[]{:S(2)}, u32[]{:S(2)}) collective-permute-start(bf16[1,320,4,128]{3,1,2,0:T(8,128)(2,1)S(1)} %get-tuple-element.5), channel_id=1, source_target_pairs={{0,8},{8,16},{16,24},{1,9},{9,17},{17,25},{2,10},{10,18},{18,26},{... | collective-permute-start | bytes 983048 | tf_op jit(solution)/shard_map/ppermute | solution.py:25
  114.8 0.5 fusion.59
  115.4 3.4 %collective-permute-done.4 = bf16[1,320,4,128]{3,1,2,0:T(8,128)(2,1)S(1)} collective-permute-done((bf16[1,320,4,128]{3,1,2,0:T(8,128)(2,1)S(1)}, bf16[1,320,4,128]{3,1,2,0:T(8,128)(2,1)S(1)}, u32[]{:S(2)}, u32[]{:S(2)}) %collective-permute-start.4) | collective-permute-done | bytes 327712 | tf_op jit(solution)/shard_map/ppermute | solution.py:27
  118.7 0.5 fusion.41
  119.3 3.6 %collective-permute-done.3 = bf16[1,320,4,128]{3,1,2,0:T(8,128)(2,1)S(1)} collective-permute-done((bf16[1,320,4,128]{3,1,2,0:T(8,128)(2,1)S(1)}, bf16[1,320,4,128]{3,1,2,0:T(8,128)(2,1)S(1)}, u32[]{:S(2)}, u32[]{:S(2)}) %collective-permute-start.3) | collective-permute-done | bytes 327712 | tf_op jit(solution)/shard_map/ppermute | solution.py:25
  122.8 0.6 fusion.17
  123.5 1.3 %copy.75 = bf16[2,320,4,128]{3,2,1,0:T(4,128)(2,1)} copy(bf16[2,320,4,128]{3,1,2,0:T(8,128)(2,1)S(1)} %fusion.17) | data formatting | bytes 1310720 | tf_op jit(solution)/shard_map/convert_element_type | solution.py:114
  (27 shorter events, 0.2 us)
Async XLA Ops:
  6.5 27.4 %copy-start = (bf16[3,1280,320]{1,2,0:T(8,128)(2,1)S(1)}, bf16[3,1280,320]{1,2,0:T(8,128)(2,1)}, u32[]{:S(2)}) copy-start(bf16[3,1280,320]{1,2,0:T(8,128)(2,1)} %param.11) | copy-start | bytes 7372804
  6.5 57.9 %reduce-scatter.4.cloned.1.call-start = ((), (), s32[]{:S(2)}) async-start(), calls=%async_computation.1 | async-start | bytes 819200
  42.5 25.3 %copy-start.4 = (bf16[320,320]{1,0:T(8,128)(2,1)S(1)}, bf16[320,320]{1,0:T(8,128)(2,1)}, u32[]{:S(2)}) copy-start(bf16[320,320]{1,0:T(8,128)(2,1)} %param.13) | copy-start | bytes 614404
  42.5 25.3 %copy-start.5 = (bf16[4,8,320]{2,1,0:T(8,128)(2,1)S(1)}, bf16[4,8,320]{2,1,0:T(8,128)(2,1)}, u32[]{:S(2)}) copy-start(bf16[4,8,320]{2,1,0:T(8,128)(2,1)} %param.10) | copy-start | bytes 61444
  66.5 23.5 %copy-start.1 = (bf16[2,320,4,128]{3,2,1,0:T(4,128)(2,1)S(1)}, bf16[2,320,4,128]{3,2,1,0:T(4,128)(2,1)}, u32[]{:S(2)}) copy-start(bf16[2,320,4,128]{3,2,1,0:T(4,128)(2,1)} %param.9) | copy-start | bytes 1966084
  68.0 22.1 %copy-start.6 = (f32[320]{0:T(512)S(1)}, f32[320]{0:T(512)}, u32[]{:S(2)}) copy-start(f32[320]{0:T(512)} %param.14) | copy-start | bytes 3844
  80.8 7.0 %collective-permute-start = (bf16[4,8,320]{2,1,0:T(8,128)(2,1)S(1)}, bf16[4,8,320]{2,1,0:T(8,128)(2,1)S(1)}, u32[]{:S(2)}, u32[]{:S(2)}) collective-permute-start(bf16[4,8,320]{2,1,0:T(8,128)(2,1)S(1)} %psum.7), channel_id=1, source_target_pairs={{0,1},{1,0},{2,3},{3,2},{4,5},{5,4},{6,7},{7,6},{8,9},{9,8},{10,11... | collective-permute-start | bytes 61448 | tf_op jit(solution)/shard_map/ppermute | solution.py:14
  90.1 5.8 %copy-start.2 = (bf16[3,3,320,320]{3,2,1,0:T(8,128)(2,1)S(1)}, bf16[3,3,320,320]{3,2,1,0:T(8,128)(2,1)}, u32[]{:S(2)}) copy-start(bf16[3,3,320,320]{3,2,1,0:T(8,128)(2,1)} %param.15) | copy-start | bytes 5529604
  90.7 5.8 %collective-permute-start.1 = (bf16[2,320,1,128]{3,1,2,0:T(8,128)(2,1)S(1)}, bf16[2,320,1,128]{3,1,2,0:T(8,128)(2,1)S(1)}, u32[]{:S(2)}, u32[]{:S(2)}) collective-permute-start(bf16[2,320,1,128]{3,1,2,0:T(8,128)(2,1)S(1)} %get-tuple-element.7), channel_id=1, source_target_pairs={{0,1},{1,2},{2,3},{3,4},{4,5},{5,6},{6,7},{8,9},{9,10},{10,11},{11... | collective-permute-start | bytes 491528 | tf_op jit(solution)/shard_map/ppermute | solution.py:25
  94.0 7.5 %collective-permute-start.2 = (bf16[2,320,1,128]{3,1,2,0:T(8,128)(2,1)S(1)}, bf16[2,320,1,128]{3,1,2,0:T(8,128)(2,1)S(1)}, u32[]{:S(2)}, u32[]{:S(2)}) collective-permute-start(bf16[2,320,1,128]{3,1,2,0:T(8,128)(2,1)S(1)} %get-tuple-element.8), channel_id=1, source_target_pairs={{1,0},{2,1},{3,2},{4,3},{5,4},{6,5},{7,6},{9,8},{10,9},{11,10},{12... | collective-permute-start | bytes 491528 | tf_op jit(solution)/shard_map/ppermute | solution.py:27
  106.6 1.0 copy-start.7
  107.6 7.2 %copy-start.3 = (bf16[3,320,320]{2,1,0:T(8,128)(2,1)S(1)}, bf16[3,320,320]{2,1,0:T(8,128)(2,1)}, u32[]{:S(2)}) copy-start(bf16[3,320,320]{2,1,0:T(8,128)(2,1)} %param.17) | copy-start | bytes 1843204
  108.2 10.6 %collective-permute-start.4 = (bf16[1,320,4,128]{3,1,2,0:T(8,128)(2,1)S(1)}, bf16[1,320,4,128]{3,1,2,0:T(8,128)(2,1)S(1)}, u32[]{:S(2)}, u32[]{:S(2)}) collective-permute-start(bf16[1,320,4,128]{3,1,2,0:T(8,128)(2,1)S(1)} %get-tuple-element.6), channel_id=1, source_target_pairs={{8,0},{16,8},{24,16},{9,1},{17,9},{25,17},{10,2},{18,10},{26,18},{... | collective-permute-start | bytes 983048 | tf_op jit(solution)/shard_map/ppermute | solution.py:27
  112.9 9.9 %collective-permute-start.3 = (bf16[1,320,4,128]{3,1,2,0:T(8,128)(2,1)S(1)}, bf16[1,320,4,128]{3,1,2,0:T(8,128)(2,1)S(1)}, u32[]{:S(2)}, u32[]{:S(2)}) collective-permute-start(bf16[1,320,4,128]{3,1,2,0:T(8,128)(2,1)S(1)} %get-tuple-element.5), channel_id=1, source_target_pairs={{0,8},{8,16},{16,24},{1,9},{9,17},{17,25},{2,10},{10,18},{18,26},{... | collective-permute-start | bytes 983048 | tf_op jit(solution)/shard_map/ppermute | solution.py:25
Sparse Core Ops, SparseCore 0:
  42.6 21.7 reduce-scatter.3
where the time goes:
time: 133 us; the launch traced here: 132 us
  blocking collectives  37.4 us (28%)
  waiting for transfers between devices  34.7 us (26%)
  starting transfers between devices  18.1 us (14%)
  local copies, waits for them, and re-layouts  15.2 us (11%)
  between operations  13.7 us (10%)
  matrix products  10.4 us (8%)
  other arithmetic  2.09 us (2%)
    all_gather x1, blocking collectives, local(): lax.all_gather(coarse, 'frame', axis=2, tiled=True)  24.7 us
    unnamed x2, waiting for transfers between devices  21.9 us
    psum x1, blocking collectives, local(): up_cells = lax.psum(up_partial, 'frame').astype(jnp.bfloat16)  12.8 us
    unnamed x21, local copies, waits for them, and re-layouts  9.83 us
    ppermute x2, waiting for transfers between devices, with_halo(): lax.ppermute(head, axis, [((i + 1) % count, i) for i in range(ends)])  8.43 us
    ppermute x2, starting transfers between devices, with_halo(): lax.ppermute(head, axis, [((i + 1) % count, i) for i in range(ends)])  6.64 us
    ppermute x1, starting transfers between devices, from_partner(): return lax.ppermute(value, axis, pairs)  6.13 us
    dot_general x9, matrix products, convolve_space(): jnp.einsum('fcrw,cd->fdrw', window, conv_space[offset_y, offset_x], prefe...  5.52 us
  transfers between devices with their start and end apart: 6, of which 5 were waited for; matrix products, arithmetic and copies ran while one was open for 1% of the time, Pallas kernels for 0%

commit v1 on v0

v1 whole, which is shorter than its diff:
```python
import functools
import math

import jax
import jax.numpy as jnp
from jax import lax
from jax.experimental import pallas as pl
from jax.experimental.pallas import tpu as pltpu
from jax.sharding import PartitionSpec as P

HD = 80
UPSAMPLE = 8
MESH = pl.DeviceIdType.MESH
BF = jnp.bfloat16
F32 = jnp.float32


def silu(a):
    half = 0.5 * a
    return half + half * jnp.tanh(half)


def dot(a, b):
    return jnp.dot(a, b, preferred_element_type=F32)


def dot_t(a, b):
    return lax.dot_general(a, b, (((0,), (0,)), ((), ())), preferred_element_type=F32)


def kernel(
    nf, nr, cf_count, p_dev,
    fine_ref, coarse_ref, w_qkv_ref, w_out_ref, w_up_ref, gain_one_ref, conv_s_ref, gain_two_ref, conv_t_ref,
    out_ref,
    wq, wo, wu, cs, ct, cst, ctt, fb, cg, rs_send, rs_recv, up_send, up_recv, ub_send, ub, x3, n2,
    load_sem, halo_send, halo_recv, g_send, g_recv, r_send, r_recv, u_send, u_recv, b_send, b_recv,
):
    f_dev, rows, chans, width = fine_ref.shape
    cells, c_dev = coarse_ref.shape
    frames_ext = f_dev + 2
    rows_ext = rows + 2
    group = (width // UPSAMPLE) // p_dev
    n_groups = nr // group
    heads = c_dev // HD
    me_f = lax.axis_index("frame")
    me_r = lax.axis_index("row")
    my_group = me_r // group
    k_me = me_r % group
    first = k_me == 0
    last = k_me == group - 1

    loads = [
        pltpu.make_async_copy(src, dst, load_sem.at[n])
        for n, (src, dst) in enumerate(
            (
                (w_qkv_ref, wq),
                (w_out_ref, wo),
                (w_up_ref, wu),
                (conv_s_ref, cs),
                (conv_t_ref, ct),
                (fine_ref, fb.at[pl.ds(1, f_dev), pl.ds(1, rows)]),
            )
        )
    ]
    for load in loads:
        load.start()

    def dev(f, r):
        return {"frame": f, "row": r}

    barrier = pltpu.get_barrier_semaphore()
    expected = jnp.int32(nf - 1)
    for step in range(1, nf):
        pl.semaphore_signal(barrier, inc=1, device_id=dev((me_f + step) % nf, me_r), device_id_type=MESH)
    row_start = my_group * group - group
    for step in range(3 * group):
        peer = row_start + step
        ok = (peer >= 0) & (peer < nr) & (peer != me_r)
        expected = expected + ok.astype(jnp.int32)

        @pl.when(ok)
        def _(peer=peer):
            pl.semaphore_signal(barrier, inc=1, device_id=dev(me_f, peer), device_id_type=MESH)

    for df in (-1, 1):
        for dr in (-1, 1):
            f, r = me_f + df, me_r + dr
            ok = (f >= 0) & (f < nf) & (r >= 0) & (r < nr)
            expected = expected + ok.astype(jnp.int32)

            @pl.when(ok)
            def _(f=f, r=r):
                pl.semaphore_signal(barrier, inc=1, device_id=dev(f, r), device_id_type=MESH)

    cg[me_f] = coarse_ref[...]
    pl.semaphore_wait(barrier, expected)

    def gather_copy(step):
        return pltpu.make_async_remote_copy(
            src_ref=coarse_ref,
            dst_ref=cg.at[me_f],
            send_sem=g_send.at[step - 1],
            recv_sem=g_recv.at[step - 1],
            device_id=dev((me_f + step) % nf, me_r),
            device_id_type=MESH,
        )

    for step in range(1, nf):
        gather_copy(step).start()

    def halo(n, df, dr):
        src_f = pl.ds(0, f_dev) if df == 0 else pl.ds(f_dev - 1 if df > 0 else 0, 1)
        dst_f = pl.ds(1, f_dev) if df == 0 else pl.ds(0 if df > 0 else frames_ext - 1, 1)
        src_r = pl.ds(0, rows) if dr == 0 else pl.ds(rows - 1 if dr > 0 else 0, 1)
        dst_r = pl.ds(1, rows) if dr == 0 else pl.ds(0 if dr > 0 else rows_ext - 1, 1)
        copy = pltpu.make_async_remote_copy(
            src_ref=fine_ref.at[src_f, src_r],
            dst_ref=fb.at[dst_f, dst_r],
            send_sem=halo_send.at[n],
            recv_sem=halo_recv.at[n],
            device_id=dev(me_f + df, me_r + dr),
            device_id_type=MESH,
        )
        there = (me_f + df >= 0) & (me_f + df < nf) & (me_r + dr >= 0) & (me_r + dr < nr)
        source = (me_f - df >= 0) & (me_f - df < nf) & (me_r - dr >= 0) & (me_r - dr < nr)
        return copy, there, source, (dst_f, dst_r)

    offsets = [(df, dr) for df in (-1, 1, 0) for dr in (0, -1, 1) if (df, dr) != (0, 0)]
    for n, (df, dr) in enumerate(offsets):
        copy, there, source, (dst_f, dst_r) = halo(n, df, dr)

        @pl.when(there)
        def _(copy=copy):
            copy.start()

        @pl.when(jnp.logical_not(source))
        def _(dst_f=dst_f, dst_r=dst_r):
            fb[dst_f, dst_r] = jnp.zeros((dst_f.size, dst_r.size, chans, width), BF)

    @pl.when(me_r == 0)
    def _():
        ub[1] = jnp.zeros(ub.shape[1:], BF)

    @pl.when(me_r == nr - 1)
    def _():
        ub[2] = jnp.zeros(ub.shape[1:], BF)

    loads[3].wait()
    loads[4].wait()
    for dy in range(3):
        cst[dy] = cs[dy].T
    ctt[...] = ct[...].T

    loads[0].wait()
    for step in range(1, nf):
        gather_copy(step).wait()
    qkv = []
    for i in range(3):
        total = None
        for j in range(nf):
            term = dot(cg[j], wq[i, j * c_dev : (j + 1) * c_dev, :])
            total = term if total is None else total + term
        qkv.append(total.astype(BF))
    query, keys, values = qkv

    head_of_lane = lax.broadcasted_iota(jnp.int32, (cells, c_dev), 1) // HD
    spread = jnp.concatenate(
        [jnp.where(head_of_lane == h, query.astype(F32), 0.0) for h in range(heads)], axis=0
    ).astype(BF)
    scores = lax.dot_general(
        spread, keys, (((1,), (1,)), ((), ())), preferred_element_type=F32
    ) / math.sqrt(HD)
    cell_q = lax.broadcasted_iota(jnp.int32, scores.shape, 0) % p_dev
    cell_k = lax.broadcasted_iota(jnp.int32, scores.shape, 1) % p_dev
    same = cell_q == cell_k
    scores = jnp.where(same, scores, -1e30)
    top = jnp.max(scores, axis=1, keepdims=True)
    weight = jnp.where(same, jnp.exp(scores - top), 0.0)
    probs = (weight / jnp.sum(weight, axis=1, keepdims=True)).astype(BF)
    mixed = dot(probs, values)
    attn = None
    for h in range(heads):
        part = jnp.where(head_of_lane == h, mixed[h * cells : (h + 1) * cells], 0.0)
        attn = part if attn is None else attn + part
    attn = attn.astype(BF)

    loads[1].wait()
    partial_out = dot(attn, wo[...])
    for j in range(nf):
        rs_send[j] = partial_out[:, j * c_dev : (j + 1) * c_dev].astype(BF)

    def scatter_copy(step):
        peer = (me_f + step) % nf
        return pltpu.make_async_remote_copy(
            src_ref=rs_send.at[peer],
            dst_ref=rs_recv.at[me_f],
            send_sem=r_send.at[step - 1],
            recv_sem=r_recv.at[step - 1],
            device_id=dev(peer, me_r),
            device_id_type=MESH,
        )

    for step in range(1, nf):
        scatter_copy(step).start()
    rs_recv[me_f] = rs_send[me_f]
    loads[2].wait()
    for step in range(1, nf):
        scatter_copy(step).wait()
    share = coarse_ref[...].astype(F32)
    for j in range(nf):
        share = share + rs_recv[j].astype(F32)
    up_partial = dot(share.astype(BF), wu[...]).astype(BF)

    up_send[...] = up_partial
    up_recv[me_f] = up_partial

    def sum_copy(step):
        return pltpu.make_async_remote_copy(
            src_ref=up_send,
            dst_ref=up_recv.at[me_f],
            send_sem=u_send.at[step - 1],
            recv_sem=u_recv.at[step - 1],
            device_id=dev((me_f + step) % nf, me_r),
            device_id_type=MESH,
        )

    for step in range(1, nf):
        sum_copy(step).start()
    for step in range(1, nf):
        sum_copy(step).wait()
    up = up_recv[0].astype(F32)
    for j in range(1, nf):
        up = up + up_recv[j].astype(F32)
    up = up.astype(BF)

    ub_send[...] = up
    ub[0, k_me] = up

    def row_copy(n, region, peer):
        return pltpu.make_async_remote_copy(
            src_ref=ub_send,
            dst_ref=ub.at[region, k_me],
            send_sem=b_send.at[n],
            recv_sem=b_recv.at[region, k_me],
            device_id=dev(me_f, peer),
            device_id_type=MESH,
        )

    def row_arrival(region, k):
        return pltpu.make_async_remote_copy(
            src_ref=ub_send,
            dst_ref=ub.at[region, k],
            send_sem=b_send.at[0],
            recv_sem=b_recv.at[region, k],
            device_id=dev(me_f, me_r),
            device_id_type=MESH,
        )

    base = my_group * group
    targets = [(step - 1, 0, base + (k_me + step) % group, None) for step in range(1, group)]
    targets.append((group - 1, 1, base + group, my_group < n_groups - 1))
    targets.append((group, 2, base - 1, my_group > 0))
    for n, region, peer, ok in targets:
        if ok is None:
            row_copy(n, region, peer).start()
        else:

            @pl.when(ok)
            def _(n=n, region=region, peer=peer):
                row_copy(n, region, peer).start()

    for step in range(1, group):
        row_arrival(0, (k_me + step) % group).wait_recv()

    @pl.when(first & (my_group > 0))
    def _():
        for k in range(group):
            row_arrival(1, k).wait_recv()

    @pl.when(last & (my_group < n_groups - 1))
    def _():
        for k in range(group):
            row_arrival(2, k).wait_recv()

    loads[5].wait()
    for n, (df, dr) in enumerate(offsets):
        copy, there, source, _ = halo(n, df, dr)

        @pl.when(there)
        def _(copy=copy):
            copy.wait_send()

        @pl.when(source)
        def _(copy=copy):
            copy.wait_recv()

    span = group * cells
    lanes = frames_ext * width
    rho = lax.broadcasted_iota(jnp.int32, (span, lanes), 0)
    lane = lax.broadcasted_iota(jnp.int32, (span, lanes), 1)
    total_frames = nf * f_dev
    frame_at = me_f * f_dev - 1 + lane // width
    wanted_frame = (frame_at * cf_count + total_frames) // total_frames - 1
    wanted_cell = (lane % width) // UPSAMPLE
    frame_of = (rho % cells) // p_dev
    cell_of = (rho // cells) * p_dev + rho % p_dev
    pick = jnp.where((wanted_frame == frame_of) & (wanted_cell == cell_of), 1.0, 0.0).astype(BF)

    def widened(region):
        block = [ub[region, k] for k in range(group)]
        block = jnp.concatenate(block, axis=0) if group > 1 else block[0]
        return dot_t(block, pick)

    own = widened(0)
    above = widened(jnp.where(first, 1, 0))
    below = widened(jnp.where(last, 2, 0))
    gain_one = gain_one_ref[...]
    gain_two = gain_two_ref[...]
    column = lax.broadcasted_iota(jnp.int32, (chans, width), 1)
    for t in range(frames_ext):
        window = slice(t * width, (t + 1) * width)
        for r in range(rows_ext):
            spread_up = above if r == 0 else below if r == rows_ext - 1 else own
            merged = (fb[t, r].astype(F32) + spread_up[:, window]).astype(BF)
            if 0 < t < frames_ext - 1 and 0 < r < rows_ext - 1:
                fb[t, r] = merged
            v = merged.astype(F32)
            scale = lax.rsqrt(jnp.mean(v * v, axis=0, keepdims=True) + 1e-06)
            act = silu(v * scale * gain_one)
            here = slice(r * width, (r + 1) * width)
            x3[t % 2, chans : 2 * chans, here] = act.astype(BF)
            left = jnp.where(column == 0, 0.0, pltpu.roll(act, 1, 1))
            right = jnp.where(column == width - 1, 0.0, pltpu.roll(act, width - 1, 1))
            x3[t % 2, 0:chans, here] = left.astype(BF)
            x3[t % 2, 2 * chans : 3 * chans, here] = right.astype(BF)
        spatial = None
        for dy in range(3):
            term = dot(cst[dy], x3[t % 2, :, dy * width : (dy + rows) * width])
            spatial = term if spatial is None else spatial + term
        for r in range(rows):
            here = slice(r * width, (r + 1) * width)
            v = spatial[:, here]
            scale = lax.rsqrt(jnp.mean(v * v, axis=0, keepdims=True) + 1e-06)
            n2[t * chans : (t + 1) * chans, here] = silu(v * scale * gain_two).astype(BF)
    for t in range(f_dev):
        temporal = dot(ctt[...], n2[t * chans : (t + 3) * chans, :])
        for r in range(rows):
            here = slice(r * width, (r + 1) * width)
            out_ref[t, r] = (fb[t + 1, r + 1].astype(F32) + temporal[:, here]).astype(BF)

    for n, region, peer, ok in targets:
        if ok is None:
            row_copy(n, region, peer).wait_send()
        else:

            @pl.when(ok)
            def _(n=n, region=region, peer=peer):
                row_copy(n, region, peer).wait_send()


def local(fine, coarse, w_qkv, w_out, w_up, gain_one, conv_space, gain_two, conv_time):
    nf = lax.axis_size("frame")
    nr = lax.axis_size("row")
    f_dev, chans, rows, width = fine.shape
    cf_count, p_dev, c_dev = coarse.shape
    cells = cf_count * p_dev
    cc = nf * c_dev
    group = (width // UPSAMPLE) // p_dev
    fine_t = jnp.transpose(fine, (0, 2, 1, 3))
    any_spec = pl.BlockSpec(memory_space=pl.ANY)
    vmem = pl.BlockSpec(memory_space=pltpu.VMEM)
    dma = pltpu.SemaphoreType.DMA
    out = pl.pallas_call(
        functools.partial(kernel, nf, nr, cf_count, p_dev),
        out_shape=jax.ShapeDtypeStruct((f_dev, rows, chans, width), BF),
        in_specs=[any_spec, vmem, any_spec, any_spec, any_spec, vmem, any_spec, vmem, any_spec],
        out_specs=vmem,
        scratch_shapes=[
            pltpu.VMEM((3, cc, c_dev), BF),
            pltpu.VMEM((c_dev, cc), BF),
            pltpu.VMEM((c_dev, chans), BF),
            pltpu.VMEM((3, 3 * chans, chans), BF),
            pltpu.VMEM((3 * chans, chans), BF),
            pltpu.VMEM((3, chans, 3 * chans), BF),
            pltpu.VMEM((chans, 3 * chans), BF),
            pltpu.VMEM((f_dev + 2, rows + 2, chans, width), BF),
            pltpu.VMEM((nf, cells, c_dev), BF),
            pltpu.VMEM((nf, cells, c_dev), BF),
            pltpu.VMEM((nf, cells, c_dev), BF),
            pltpu.VMEM((cells, chans), BF),
            pltpu.VMEM((nf, cells, chans), BF),
            pltpu.VMEM((cells, chans), BF),
            pltpu.VMEM((3, group, cells, chans), BF),
            pltpu.VMEM((2, 3 * chans, (rows + 2) * width), BF),
            pltpu.VMEM(((f_dev + 2) * chans, rows * width), BF),
            dma((6,)),
            dma((8,)),
            dma((8,)),
            dma((nf,)),
            dma((nf,)),
            dma((nf,)),
            dma((nf,)),
            dma((nf,)),
            dma((nf,)),
            dma((group + 1,)),
            dma((3, group)),
        ],
        compiler_params=pltpu.CompilerParams(
            collective_id=0, has_side_effects=True, vmem_limit_bytes=56 * 1024 * 1024
        ),
        name="decoder_window",
    )(
        fine_t,
        coarse.reshape(cells, c_dev),
        w_qkv,
        w_out,
        w_up,
        jnp.broadcast_to(gain_one[:, None], (chans, width)),
        conv_space.reshape(3, 3 * chans, chans),
        jnp.broadcast_to(gain_two[:, None], (chans, width)),
        conv_time.reshape(3 * chans, chans),
    )
    return jnp.transpose(out, (0, 2, 1, 3))


def solution(mesh):
    return jax.shard_map(
        local,
        mesh=mesh,
        in_specs=(
            P("frame", None, "row", None),
            P(None, "row", "frame"),
            P(None, None, "frame"),
            P("frame", None),
            P("frame", None),
            P(),
            P(),
            P(),
            P(),
        ),
        out_specs=P("frame", None, "row", None),
        check_vma=False,
    )
```

time: 133 us -> 52.6 us (0.40)
  the two profiles are of different devices: /device:TPU:11 before, /device:TPU:1 now
where the time goes in v1:
time: 52.6 us; the launch traced here: 52.2 us
  Pallas kernels  39.6 us (75%)
  local copies, waits for them, and re-layouts  12.6 us (24%)
    pallas_call x1, Pallas kernels, local(): pl.pallas_call(functools.partial(kernel, nf, nr, cf_count, p_dev), out_sh...  39.6 us
    unnamed x2, local copies, waits for them, and re-layouts  7.27 us
    transpose x1, local copies, waits for them, and re-layouts, local(): return jnp.transpose(out, (0, 2, 1, 3))  2.43 us
    broadcast_in_dim x1, local copies, waits for them, and re-layouts, local(): jnp.broadcast_to(gain_two[:, None], (chans, width))  1.46 us
    broadcast_in_dim x1, local copies, waits for them, and re-layouts, local(): jnp.broadcast_to(gain_one[:, None], (chans, width))  1.44 us

profile of v1, /device:TPU:1, one launch (start us, length us, event | category | flops | bytes accessed | tf_op | source)
XLA Modules:
  0.0 52.2 jit_solution(15162667790956660847)
XLA Ops:
  0.0 1.4 %broadcast_in_dim.4.gain_one_ref = f32[320,128]{1,0:T(8,128)} broadcast(f32[320]{0:T(512)} %param.14), dimensions={0} | broadcast | bytes 165120 | tf_op jit(solution)/shard_map/broadcast_in_dim | solution.py:418
  1.4 1.5 %broadcast_in_dim.5.gain_two_ref = f32[320,128]{1,0:T(8,128)} broadcast(f32[320]{0:T(512)} %param.16), dimensions={0} | broadcast | bytes 165120 | tf_op jit(solution)/shard_map/broadcast_in_dim | solution.py:420
  2.9 2.0 %copy.14 = bf16[2,320,4,128]{3,1,2,0:T(8,128)(2,1)} copy(bf16[2,320,4,128]{3,2,1,0:T(4,128)(2,1)} %param.9) | data formatting | bytes 1310720 | tf_op args[0]
  4.9 5.3 %copy.11.w_qkv_ref = bf16[3,1280,320]{2,1,0:T(8,128)(2,1)} copy(bf16[3,1280,320]{1,2,0:T(8,128)(2,1)} %param.11) | data formatting | bytes 4915200 | tf_op args[2]
  10.2 39.6 %decoder_window.1 = bf16[2,4,320,128]{3,2,1,0:T(8,128)(2,1)} custom-call(bf16[2,4,320,128]{3,2,1,0:T(8,128)(2,1)} %bitcast.8, bf16[32,320]{1,0:T(8,128)(2,1)} %bitcast.11, bf16[3,1280,320]{2,1,0:T(8,128)(2,1)} %copy.11.w_qkv_ref, bf16[320,1280]{1,0:T(8,128)(2,1)} %w_out_ref.1, bf16[320,320]{1,0:T(8,128)(2,1)} %w_up_ref.1, ...), custom_call_target="tpu_custom_call" | custom-call | tf_op jit(solution)/shard_map/decoder_window/pallas_call | solution.py:373
  49.8 2.4 %copy.12 = bf16[2,320,4,128]{3,2,1,0:T(4,128)(2,1)} copy(bf16[2,320,4,128]{3,1,2,0:T(8,128)(2,1)} %bitcast.7) | data formatting | bytes 1310720 | tf_op jit(solution)/shard_map/transpose | solution.py:423

commit v2 on v1

--- a/solution.py
+++ b/solution.py
@@ -32,7 +32,7 @@
     nf, nr, cf_count, p_dev,
     fine_ref, coarse_ref, w_qkv_ref, w_out_ref, w_up_ref, gain_one_ref, conv_s_ref, gain_two_ref, conv_t_ref,
     out_ref,
-    wq, wo, wu, cs, ct, cst, ctt, fb, cg, rs_send, rs_recv, up_send, up_recv, ub_send, ub, x3, n2,
+    wq, wo, wu, cs, ct, cst, ctt, fb, cg, rs_send, rs_recv, up_send, up_recv, ub_send, ub, x3, n2, gain_one, gain_two,
     load_sem, halo_send, halo_recv, g_send, g_recv, r_send, r_recv, u_send, u_recv, b_send, b_recv,
 ):
     f_dev, rows, chans, width = fine_ref.shape
@@ -49,20 +49,21 @@
     first = k_me == 0
     last = k_me == group - 1
 
-    loads = [
-        pltpu.make_async_copy(src, dst, load_sem.at[n])
-        for n, (src, dst) in enumerate(
-            (
-                (w_qkv_ref, wq),
-                (w_out_ref, wo),
-                (w_up_ref, wu),
-                (conv_s_ref, cs),
-                (conv_t_ref, ct),
-                (fine_ref, fb.at[pl.ds(1, f_dev), pl.ds(1, rows)]),
-            )
-        )
-    ]
-    for load in loads:
+    parts = {
+        "space0": (conv_s_ref.at[0], cs.at[0]),
+        "qkv": (w_qkv_ref, wq),
+        "out": (w_out_ref, wo),
+        "space1": (conv_s_ref.at[1], cs.at[1]),
+        "up": (w_up_ref, wu),
+        "space2": (conv_s_ref.at[2], cs.at[2]),
+        "time": (conv_t_ref, ct),
+        "fine": (fine_ref, fb.at[pl.ds(1, f_dev), pl.ds(1, rows)]),
+    }
+    loads = {
+        name: pltpu.make_async_copy(src, dst, load_sem.at[n])
+        for n, (name, (src, dst)) in enumerate(parts.items())
+    }
+    for load in loads.values():
         load.start()
 
     def dev(f, r):
@@ -82,16 +83,6 @@
         def _(peer=peer):
             pl.semaphore_signal(barrier, inc=1, device_id=dev(me_f, peer), device_id_type=MESH)
 
-    for df in (-1, 1):
-        for dr in (-1, 1):
-            f, r = me_f + df, me_r + dr
-            ok = (f >= 0) & (f < nf) & (r >= 0) & (r < nr)
-            expected = expected + ok.astype(jnp.int32)
-
-            @pl.when(ok)
-            def _(f=f, r=r):
-                pl.semaphore_signal(barrier, inc=1, device_id=dev(f, r), device_id_type=MESH)
-
     cg[me_f] = coarse_ref[...]
     pl.semaphore_wait(barrier, expected)
 
@@ -108,34 +99,85 @@
     for step in range(1, nf):
         gather_copy(step).start()
 
-    def halo(n, df, dr):
-        src_f = pl.ds(0, f_dev) if df == 0 else pl.ds(f_dev - 1 if df > 0 else 0, 1)
-        dst_f = pl.ds(1, f_dev) if df == 0 else pl.ds(0 if df > 0 else frames_ext - 1, 1)
-        src_r = pl.ds(0, rows) if dr == 0 else pl.ds(rows - 1 if dr > 0 else 0, 1)
-        dst_r = pl.ds(1, rows) if dr == 0 else pl.ds(0 if dr > 0 else rows_ext - 1, 1)
-        copy = pltpu.make_async_remote_copy(
-            src_ref=fine_ref.at[src_f, src_r],
-            dst_ref=fb.at[dst_f, dst_r],
+    def remote(n, src, dst, f, r):
+        return pltpu.make_async_remote_copy(
+            src_ref=src,
+            dst_ref=dst,
             send_sem=halo_send.at[n],
             recv_sem=halo_recv.at[n],
-            device_id=dev(me_f + df, me_r + dr),
-            device_id_type=MESH,
-        )
-        there = (me_f + df >= 0) & (me_f + df < nf) & (me_r + dr >= 0) & (me_r + dr < nr)
-        source = (me_f - df >= 0) & (me_f - df < nf) & (me_r - dr >= 0) & (me_r - dr < nr)
-        return copy, there, source, (dst_f, dst_r)
-
-    offsets = [(df, dr) for df in (-1, 1, 0) for dr in (0, -1, 1) if (df, dr) != (0, 0)]
-    for n, (df, dr) in enumerate(offsets):
-        copy, there, source, (dst_f, dst_r) = halo(n, df, dr)
-
-        @pl.when(there)
-        def _(copy=copy):
-            copy.start()
+            device_id=dev(f, r),
+            device_id_type=MESH,
+        )
+
+    own_f, own_r = pl.ds(1, f_dev), pl.ds(1, rows)
+    cut = (rows + 1) // 2
+    pieces = [(0, cut), (cut, rows - cut)]
+    row_halo, frame_halo, corner_halo = [], [[], []], []
+    for n, d in enumerate((-1, 1)):
+        there = (me_r + d >= 0) & (me_r + d < nr)
+        source = (me_r - d >= 0) & (me_r - d < nr)
+        src_r, dst_r = (rows - 1, 0) if d > 0 else (0, rows_ext - 1)
+        row_halo.append(
+            (
+                remote(n, fine_ref.at[:, pl.ds(src_r, 1)], fb.at[own_f, pl.ds(dst_r, 1)], me_f, me_r + d),
+                there,
+                source,
+            )
+        )
 
         @pl.when(jnp.logical_not(source))
-        def _(dst_f=dst_f, dst_r=dst_r):
-            fb[dst_f, dst_r] = jnp.zeros((dst_f.size, dst_r.size, chans, width), BF)
+        def _(dst_r=dst_r):
+            fb[:, dst_r] = jnp.zeros((frames_ext, chans, width), BF)
+
+        for e, at in enumerate((0, frames_ext - 1)):
+            corner_halo.append(
+                (
+                    remote(6 + 2 * n + e, fb.at[at, src_r + 1], fb.at[at, dst_r], me_f, me_r + d),
+                    there & (me_f > 0 if e == 0 else me_f < nf - 1),
+                    source & (me_f > 0 if e == 0 else me_f < nf - 1),
+                )
+            )
+        there = (me_f + d >= 0) & (me_f + d < nf)
+        source = (me_f - d >= 0) & (me_f - d < nf)
+        src_f, dst_f = (f_dev - 1, 0) if d > 0 else (0, frames_ext - 1)
+        for piece, (start, size) in enumerate(pieces):
+            if size:
+                copy = remote(
+                    2 + 2 * n + piece,
+                    fine_ref.at[src_f, pl.ds(start, size)],
+                    fb.at[dst_f, pl.ds(1 + start, size)],
+                    me_f + d,
+                    me_r,
+                )
+                frame_halo[piece].append((copy, there, source))
+
+        @pl.when(jnp.logical_not(source))
+        def _(dst_f=dst_f):
+            fb[dst_f] = jnp.zeros((rows_ext, chans, width), BF)
+
+    def start_all(copies):
+        for copy, there, _ in copies:
+
+            @pl.when(there)
+            def _(copy=copy):
+                copy.start()
+
+    def arrive_all(copies):
+        for copy, _, source in copies:
+
+            @pl.when(source)
+            def _(copy=copy):
+                copy.wait_recv()
+
+    def sent_all(copies):
+        for copy, there, _ in copies:
+
+            @pl.when(there)
+            def _(copy=copy):
+                copy.wait_send()
+
+    start_all(frame_halo[0])
+    start_all(row_halo)
 
     @pl.when(me_r == 0)
     def _():
@@ -145,22 +187,24 @@
     def _():
         ub[2] = jnp.zeros(ub.shape[1:], BF)
 
-    loads[3].wait()
-    loads[4].wait()
-    for dy in range(3):
+    gain_one[...] = jnp.broadcast_to(gain_one_ref[...], (width, chans)).T
+    gain_two[...] = jnp.broadcast_to(gain_two_ref[...], (width, chans)).T
+
+    def turn(dy):
+        loads[f"space{dy}"].wait()
         cst[dy] = cs[dy].T
-    ctt[...] = ct[...].T
-
-    loads[0].wait()
+
+    turn(0)
+    loads["qkv"].wait()
     for step in range(1, nf):
         gather_copy(step).wait()
+    cells_all = jnp.concatenate([cg[j].astype(F32) for j in range(nf)], axis=1).astype(BF)
     qkv = []
     for i in range(3):
-        total = None
-        for j in range(nf):
-            term = dot(cg[j], wq[i, j * c_dev : (j + 1) * c_dev, :])
-            total = term if total is None else total + term
-        qkv.append(total.astype(BF))
+        product = lax.dot_general(
+            cells_all, wq[i], (((1,), (1,)), ((), ())), preferred_element_type=F32
+        )
+        qkv.append(product.astype(BF))
     query, keys, values = qkv
 
     head_of_lane = lax.broadcasted_iota(jnp.int32, (cells, c_dev), 1) // HD
@@ -184,7 +228,7 @@
         attn = part if attn is None else attn + part
     attn = attn.astype(BF)
 
-    loads[1].wait()
+    loads["out"].wait()
     partial_out = dot(attn, wo[...])
     for j in range(nf):
         rs_send[j] = partial_out[:, j * c_dev : (j + 1) * c_dev].astype(BF)
@@ -203,7 +247,8 @@
     for step in range(1, nf):
         scatter_copy(step).start()
     rs_recv[me_f] = rs_send[me_f]
-    loads[2].wait()
+    turn(1)
+    loads["up"].wait()
     for step in range(1, nf):
         scatter_copy(step).wait()
     share = coarse_ref[...].astype(F32)
@@ -226,6 +271,8 @@
 
     for step in range(1, nf):
         sum_copy(step).start()
+    start_all(frame_halo[1])
+    turn(2)
     for step in range(1, nf):
         sum_copy(step).wait()
     up = up_recv[0].astype(F32)
@@ -269,31 +316,8 @@
             def _(n=n, region=region, peer=peer):
                 row_copy(n, region, peer).start()
 
-    for step in range(1, group):
-        row_arrival(0, (k_me + step) % group).wait_recv()
-
-    @pl.when(first & (my_group > 0))
-    def _():
-        for k in range(group):
-            row_arrival(1, k).wait_recv()
-
-    @pl.when(last & (my_group < n_groups - 1))
-    def _():
-        for k in range(group):
-            row_arrival(2, k).wait_recv()
-
-    loads[5].wait()
-    for n, (df, dr) in enumerate(offsets):
-        copy, there, source, _ = halo(n, df, dr)
-
-        @pl.when(there)
-        def _(copy=copy):
-            copy.wait_send()
-
-        @pl.when(source)
-        def _(copy=copy):
-            copy.wait_recv()
-
+    loads["time"].wait()
+    ctt[...] = ct[...].T
     span = group * cells
     lanes = frames_ext * width
     rho = lax.broadcasted_iota(jnp.int32, (span, lanes), 0)
@@ -306,6 +330,21 @@
     cell_of = (rho // cells) * p_dev + rho % p_dev
     pick = jnp.where((wanted_frame == frame_of) & (wanted_cell == cell_of), 1.0, 0.0).astype(BF)
 
+    loads["fine"].wait()
+    arrive_all(row_halo)
+    for step in range(1, group):
+        row_arrival(0, (k_me + step) % group).wait_recv()
+
+    @pl.when(first & (my_group > 0))
+    def _():
+        for k in range(group):
+            row_arrival(1, k).wait_recv()
+
+    @pl.when(last & (my_group < n_groups - 1))
+    def _():
+        for k in range(group):
+            row_arrival(2, k).wait_recv()
+
     def widened(region):
         block = [ub[region, k] for k in range(group)]
         block = jnp.concatenate(block, axis=0) if group > 1 else block[0]
@@ -314,10 +353,15 @@
     own = widened(0)
     above = widened(jnp.where(first, 1, 0))
     below = widened(jnp.where(last, 2, 0))
-    gain_one = gain_one_ref[...]
-    gain_two = gain_two_ref[...]
     column = lax.broadcasted_iota(jnp.int32, (chans, width), 1)
-    for t in range(frames_ext):
+    for place, t in enumerate([*range(1, frames_ext - 1), 0, frames_ext - 1]):
+        if place == 1:
+            arrive_all(frame_halo[0])
+            arrive_all(frame_halo[1])
+            start_all(corner_halo)
+        if t == 0:
+            arrive_all(corner_halo)
+        slot = place % 2
         window = slice(t * width, (t + 1) * width)
         for r in range(rows_ext):
             spread_up = above if r == 0 else below if r == rows_ext - 1 else own
@@ -326,28 +370,29 @@
                 fb[t, r] = merged
             v = merged.astype(F32)
             scale = lax.rsqrt(jnp.mean(v * v, axis=0, keepdims=True) + 1e-06)
-            act = silu(v * scale * gain_one)
+            act = silu(v * scale * gain_one[...])
             here = slice(r * width, (r + 1) * width)
-            x3[t % 2, chans : 2 * chans, here] = act.astype(BF)
+            x3[slot, chans : 2 * chans, here] = act.astype(BF)
             left = jnp.where(column == 0, 0.0, pltpu.roll(act, 1, 1))
             right = jnp.where(column == width - 1, 0.0, pltpu.roll(act, width - 1, 1))
-            x3[t % 2, 0:chans, here] = left.astype(BF)
-            x3[t % 2, 2 * chans : 3 * chans, here] = right.astype(BF)
+            x3[slot, 0:chans, here] = left.astype(BF)
+            x3[slot, 2 * chans : 3 * chans, here] = right.astype(BF)
         spatial = None
         for dy in range(3):
-            term = dot(cst[dy], x3[t % 2, :, dy * width : (dy + rows) * width])
+            term = dot(cst[dy], x3[slot, :, dy * width : (dy + rows) * width])
             spatial = term if spatial is None else spatial + term
         for r in range(rows):
             here = slice(r * width, (r + 1) * width)
             v = spatial[:, here]
             scale = lax.rsqrt(jnp.mean(v * v, axis=0, keepdims=True) + 1e-06)
-            n2[t * chans : (t + 1) * chans, here] = silu(v * scale * gain_two).astype(BF)
+            n2[t * chans : (t + 1) * chans, here] = silu(v * scale * gain_two[...]).astype(BF)
     for t in range(f_dev):
         temporal = dot(ctt[...], n2[t * chans : (t + 3) * chans, :])
         for r in range(rows):
             here = slice(r * width, (r + 1) * width)
             out_ref[t, r] = (fb[t + 1, r + 1].astype(F32) + temporal[:, here]).astype(BF)
 
+    sent_all([*row_halo, *frame_halo[0], *frame_halo[1], *corner_halo])
     for n, region, peer, ok in targets:
         if ok is None:
             row_copy(n, region, peer).wait_send()
@@ -376,7 +421,7 @@
         in_specs=[any_spec, vmem, any_spec, any_spec, any_spec, vmem, any_spec, vmem, any_spec],
         out_specs=vmem,
         scratch_shapes=[
-            pltpu.VMEM((3, cc, c_dev), BF),
+            pltpu.VMEM((3, c_dev, cc), BF),
             pltpu.VMEM((c_dev, cc), BF),
             pltpu.VMEM((c_dev, chans), BF),
             pltpu.VMEM((3, 3 * chans, chans), BF),
@@ -393,9 +438,11 @@
             pltpu.VMEM((3, group, cells, chans), BF),
             pltpu.VMEM((2, 3 * chans, (rows + 2) * width), BF),
             pltpu.VMEM(((f_dev + 2) * chans, rows * width), BF),
-            dma((6,)),
+            pltpu.VMEM((chans, width), F32),
+            pltpu.VMEM((chans, width), F32),
             dma((8,)),
-            dma((8,)),
+            dma((10,)),
+            dma((10,)),
             dma((nf,)),
             dma((nf,)),
             dma((nf,)),
@@ -412,12 +459,12 @@
     )(
         fine_t,
         coarse.reshape(cells, c_dev),
-        w_qkv,
+        jnp.swapaxes(w_qkv, 1, 2),
         w_out,
         w_up,
-        jnp.broadcast_to(gain_one[:, None], (chans, width)),
+        gain_one.reshape(1, chans),
         conv_space.reshape(3, 3 * chans, chans),
-        jnp.broadcast_to(gain_two[:, None], (chans, width)),
+        gain_two.reshape(1, chans),
         conv_time.reshape(3 * chans, chans),
     )
     return jnp.transpose(out, (0, 2, 1, 3))

time: 52.6 us -> 41.9 us (0.80)
  the two profiles are of different devices: /device:TPU:1 before, /device:TPU:11 now
where the time goes in v2:
time: 41.9 us; the launch traced here: 41.5 us
  Pallas kernels  34.6 us (83%)
  local copies, waits for them, and re-layouts  6.91 us (16%)
    pallas_call x1, Pallas kernels, local(): pl.pallas_call(functools.partial(kernel, nf, nr, cf_count, p_dev), out_sh...  34.6 us
    transpose x1, local copies, waits for them, and re-layouts, local(): return jnp.transpose(out, (0, 2, 1, 3))  2.43 us
    unnamed x1, local copies, waits for them, and re-layouts  2.01 us
    reshape x1, local copies, waits for them, and re-layouts, local(): gain_two.reshape(1, chans)  1.25 us
    reshape x1, local copies, waits for them, and re-layouts, local(): gain_one.reshape(1, chans)  1.22 us

profile of v2, /device:TPU:11, one launch (start us, length us, event | category | flops | bytes accessed | tf_op | source)
XLA Modules:
  0.0 41.5 jit_solution(9202648180490105236)
XLA Ops:
  0.0 1.2 %reshape.16.gain_one_ref = f32[1,320]{1,0:T(1,128)} reshape(f32[320]{0:T(512)} %param.14) | data formatting | bytes 2560 | tf_op jit(solution)/shard_map/reshape | solution.py:465
  1.2 1.2 %reshape.18.gain_two_ref = f32[1,320]{1,0:T(1,128)} reshape(f32[320]{0:T(512)} %param.16) | data formatting | bytes 2560 | tf_op jit(solution)/shard_map/reshape | solution.py:467
  2.5 2.0 %copy.13 = bf16[2,320,4,128]{3,1,2,0:T(8,128)(2,1)} copy(bf16[2,320,4,128]{3,2,1,0:T(4,128)(2,1)} %param.9) | data formatting | bytes 1310720 | tf_op args[0]
  4.5 34.6 %decoder_window.1 = bf16[2,4,320,128]{3,2,1,0:T(8,128)(2,1)} custom-call(bf16[2,4,320,128]{3,2,1,0:T(8,128)(2,1)} %bitcast.9, bf16[32,320]{1,0:T(8,128)(2,1)} %bitcast.13, bf16[3,320,1280]{2,1,0:T(8,128)(2,1)} %bitcast.10, bf16[320,1280]{1,0:T(8,128)(2,1)} %w_out_ref.1, bf16[320,320]{1,0:T(8,128)(2,1)} %w_up_ref.1, f32[1,320]{1,0:T(1,128)} %reshape.16.gain_one_ref, ...), custom_call_target="tpu_custom_call" | custom-call | tf_op jit(solution)/shard_map/decoder_window/pallas_call | solution.py:418
  39.1 2.4 %copy.11 = bf16[2,320,4,128]{3,2,1,0:T(4,128)(2,1)} copy(bf16[2,320,4,128]{3,1,2,0:T(8,128)(2,1)} %bitcast.8) | data formatting | bytes 1310720 | tf_op jit(solution)/shard_map/transpose | solution.py:470

commit v3 on v2

--- a/solution.py
+++ b/solution.py
@@ -187,8 +187,8 @@
     def _():
         ub[2] = jnp.zeros(ub.shape[1:], BF)
 
-    gain_one[...] = jnp.broadcast_to(gain_one_ref[...], (width, chans)).T
-    gain_two[...] = jnp.broadcast_to(gain_two_ref[...], (width, chans)).T
+    gain_one[...] = jnp.broadcast_to(gain_one_ref[...][None, :], (width, chans)).T
+    gain_two[...] = jnp.broadcast_to(gain_two_ref[...][None, :], (width, chans)).T
 
     def turn(dy):
         loads[f"space{dy}"].wait()
@@ -462,9 +462,9 @@
         jnp.swapaxes(w_qkv, 1, 2),
         w_out,
         w_up,
-        gain_one.reshape(1, chans),
+        gain_one,
         conv_space.reshape(3, 3 * chans, chans),
-        gain_two.reshape(1, chans),
+        gain_two,
         conv_time.reshape(3 * chans, chans),
     )
     return jnp.transpose(out, (0, 2, 1, 3))

time: 41.9 us -> 39.4 us (0.940)
  local copies, waits for them, and re-layouts: 6.91 us -> 4.44 us
    reshape x2 -> x0, local copies, waits for them, and re-layouts: 2.47 us -> none  [the longest x1 1.25 us: local(): gain_two.reshape(1, chans)]
where the time goes in v3:
time: 39.4 us; the launch traced here: 39.1 us
  Pallas kernels  34.6 us (88%)
  local copies, waits for them, and re-layouts  4.44 us (11%)
    pallas_call x1, Pallas kernels, local(): pl.pallas_call(functools.partial(kernel, nf, nr, cf_count, p_dev), out_sh...  34.6 us
    transpose x1, local copies, waits for them, and re-layouts, local(): return jnp.transpose(out, (0, 2, 1, 3))  2.43 us
    unnamed x1, local copies, waits for them, and re-layouts  2.01 us

profile of v3, /device:TPU:11, one launch (start us, length us, event | category | flops | bytes accessed | tf_op | source)
XLA Modules:
  0.0 39.1 jit_solution(6091600755456604838)
XLA Ops:
  0.0 2.0 %copy.13 = bf16[2,320,4,128]{3,1,2,0:T(8,128)(2,1)} copy(bf16[2,320,4,128]{3,2,1,0:T(4,128)(2,1)} %param.9) | data formatting | bytes 1310720 | tf_op args[0]
  2.0 34.6 %decoder_window.1 = bf16[2,4,320,128]{3,2,1,0:T(8,128)(2,1)} custom-call(bf16[2,4,320,128]{3,2,1,0:T(8,128)(2,1)} %bitcast.9, bf16[32,320]{1,0:T(8,128)(2,1)} %bitcast.13, bf16[3,320,1280]{2,1,0:T(8,128)(2,1)} %bitcast.10, bf16[320,1280]{1,0:T(8,128)(2,1)} %w_out_ref.1, bf16[320,320]{1,0:T(8,128)(2,1)} %w_up_ref.1, f32[320]{0:T(512)} %gain_one_ref.1, ...), custom_call_target="tpu_custom_call" | custom-call | tf_op jit(solution)/shard_map/decoder_window/pallas_call | solution.py:418
  36.7 2.4 %copy.11 = bf16[2,320,4,128]{3,2,1,0:T(4,128)(2,1)} copy(bf16[2,320,4,128]{3,1,2,0:T(8,128)(2,1)} %bitcast.8) | data formatting | bytes 1310720 | tf_op jit(solution)/shard_map/transpose | solution.py:470
